TPU v7x, 32 devices: a whole 2x2x4 slice. The times are simulated.
32 devices in a mesh: gx: 8 (over y, x, core), gy: 4 (over z).
Axes of the slice: x: 2, y: 2, z: 4, core: 2. Of those that a mesh axis runs over, the one named last changes fastest.
Arguments:
- point_feats: bfloat16 [262144, 128], P(('gx', 'gy')), may hold values from -6 to 6
- point_tile: int32 [262144, 1], P(('gx', 'gy')), may hold values from 0 to 31; in each aligned block of 8192 rows (0 to 8191, 8192 to 16383, ...) at most 320 rows name the same one
- point_cell: int32 [262144], P(('gx', 'gy')), may hold values from 0 to 4095
- point_count: int32 [32], P(('gx', 'gy')), may hold values from 6144 to 8192, as said below
- conv_weight: bfloat16 [3, 3, 128, 128], replicated, may hold values from -0.1875 to 0.1875
- conv_bias: float32 [128], replicated, may hold values from -3 to 3
Outputs:
- bev_map: bfloat16 [128, 1024, 128], P('gx', 'gy')
- conv_out: bfloat16 [128, 1024, 128], P('gx', 'gy')
Inputs may be any that keep to these rules, and one draw needn't show every extreme that they name: `point_tile`: among the 8192 rows of one device no tile is named by more than 320 rows, a bound that some block reaches. `point_count`: only slots below a device's count are live; some device has all 8192 slots live.
All inputs are finite; a program needn't handle non-finite values.
Results may differ from a plain program's by a relative error of at most 0.0045.
Values may be sent and summed in bfloat16 or wider, within the bound.
A program may use at most 64 MiB of HBM per device.

v0:
```python
import jax
import jax.numpy as jnp
from jax import lax
from jax.sharding import PartitionSpec as P

COLS_DEV = 256
ROWS_DEV = 16


def with_halo(cells, sides, width):
    for axis, dim in sides:
        count = lax.axis_size(axis)
        ends = count - 1
        head = lax.slice_in_dim(cells, 0, width, axis=dim)
        tail = lax.slice_in_dim(cells, cells.shape[dim] - width, cells.shape[dim], axis=dim)
        cells = jnp.concatenate(
            [
                lax.ppermute(tail, axis, [(i, (i + 1) % count) for i in range(ends)]),
                cells,
                lax.ppermute(head, axis, [((i + 1) % count, i) for i in range(ends)]),
            ],
            axis=dim,
        )
    return cells


def shards(point_feats, point_tile, point_cell, point_count, conv_weight, conv_bias):
    size_gx = lax.axis_size("gx")
    size_gy = lax.axis_size("gy")
    devices = size_gx * size_gy
    points = point_feats.shape[0]
    channels = point_feats.shape[1]
    capacity = 5 * points // (4 * devices)
    slots = devices * capacity
    target = point_tile[:, 0]
    live = jnp.arange(points, dtype=jnp.int32) < point_count[0]
    hits = (target[:, None] == jnp.arange(devices, dtype=jnp.int32)[None, :]) & live[:, None]
    blk = min(128, points)
    nblk = points // blk
    inner_idx = jnp.arange(blk, dtype=jnp.int32)
    lower = (inner_idx[:, None] >= inner_idx[None, :]).astype(jnp.bfloat16)
    hit_blocks = hits.astype(jnp.bfloat16).reshape(nblk, blk, devices)
    inner = jnp.einsum("ij,bjd->bid", lower, hit_blocks, preferred_element_type=jnp.float32)
    totals = inner[:, -1, :]
    before = jnp.cumsum(totals, axis=0) - totals
    ranks = (inner + before[:, None, :]).reshape(points, devices)
    place = jnp.sum(jnp.where(hits, ranks, 0.0), axis=1).astype(jnp.int32) - 1
    position = jnp.where(live, target * capacity + place, slots)
    slot_ids = jnp.arange(slots, dtype=jnp.int32)

    def pick(found, item):
        pos_block, first = item
        matches = pos_block[:, None] == slot_ids[None, :]
        owners = (first + inner_idx + 1)[:, None]
        return (found + jnp.sum(jnp.where(matches, owners, 0), axis=0), None)

    starts = jnp.arange(nblk, dtype=jnp.int32) * blk
    source, unused = lax.scan(
        pick, jnp.zeros((slots,), jnp.int32), (position.reshape(nblk, blk), starts)
    )
    filled = source > 0
    source_row = jnp.maximum(source - 1, 0)
    send_feats = jnp.where(
        filled[:, None], jnp.take(point_feats, source_row, axis=0), jnp.zeros((), jnp.bfloat16)
    )
    send_cells = jnp.where(filled, jnp.take(point_cell, source_row, axis=0), -1)
    got_feats, got_cells = (
        lax.all_to_all(
            send_feats.reshape(devices, capacity, channels),
            ("gx", "gy"),
            split_axis=0,
            concat_axis=0,
            tiled=True,
        ),
        lax.all_to_all(
            send_cells.reshape(devices, capacity),
            ("gx", "gy"),
            split_axis=0,
            concat_axis=0,
            tiled=True,
        ),
    )
    got_feats = got_feats.reshape(-1, channels)
    got_cells = got_cells.reshape(-1)
    col_ids = jnp.arange(COLS_DEV, dtype=jnp.int32)

    def one_row(row):
        wanted = row * COLS_DEV + col_ids
        onehot = (wanted[:, None] == got_cells[None, :]).astype(jnp.bfloat16)
        return jnp.dot(onehot, got_feats, preferred_element_type=jnp.float32)

    sums = lax.map(one_row, jnp.arange(ROWS_DEV, dtype=jnp.int32))
    bev_map = sums.astype(jnp.bfloat16)
    padded = with_halo(bev_map, (("gx", 0), ("gy", 1)), 1)
    total = jnp.zeros((ROWS_DEV, COLS_DEV, channels), jnp.float32)
    for shift_row in range(3):
        for shift_col in range(3):
            window = padded[shift_row : shift_row + ROWS_DEV, shift_col : shift_col + COLS_DEV]
            total = total + jnp.einsum(
                "rcd,de->rce",
                window,
                conv_weight[shift_row, shift_col],
                preferred_element_type=jnp.float32,
            )
    conv_out = jax.nn.relu(total + conv_bias).astype(jnp.bfloat16)
    return (bev_map, conv_out)


def solution(mesh):
    in_specs = (
        P(("gx", "gy"), None),
        P(("gx", "gy"), None),
        P(("gx", "gy")),
        P(("gx", "gy")),
        P(),
        P(),
    )
    out_specs = (P("gx", "gy", None), P("gx", "gy", None))
    return jax.shard_map(shards, mesh=mesh, in_specs=in_specs, out_specs=out_specs, check_vma=False)
```

profile of v0, /device:TPU:1, one launch (start us, length us, event | category | flops | bytes accessed | tf_op | source)
XLA Modules:
  0.0 413.7 jit_solution(5478372199037193040)
XLA Ops:
  5.0 2.9 copy.36
  9.6 2.7 select_reduce_fusion.1
  12.4 133.2 %while.25 = (s32[]{:T(128)}, s32[10240]{0:T(1024)S(1)}, s32[64,128]{1,0:T(8,128)S(1)}, s32[64]{0:T(128)S(1)}) while((s32[]{:T(128)}, s32[10240]{0:T(1024)S(1)}, s32[64,128]{1,0:T(8,128)S(1)}, s32[64]{0:T(128)S(1)}) %tuple.59), condition=%wide.region_4.5_spmd.clone.clone, body=%wide.region_2.4_spmd.clone.sunk.clone | while | flops 3942659 | bytes 166483 | solution.py:58
  145.7 56.8 %gather_fusion = s32[10240]{0:T(1024)S(1)} fusion(s32[8192]{0:T(1024)S(1)} %copy-done.1, s32[10240]{0:T(1024)S(1)} %fusion.43), kind=kCustom, calls=%fused_computation | custom fusion | bytes 122880 | tf_op jit(solution)/shard_map/jit(_take)/gather | solution.py:66
  203.2 7.1 %all-to-all-start = ((s32[32,1,320]{2,1,0:T(1,128)}), s32[32,1,320]{2,1,0:T(1,128)S(1)}, u32[]{:S(2)}, u32[]{:S(2)}) async-start(s32[32,1,320]{2,1,0:T(1,128)} %all_to_all.11), calls=%async_computation | async-start | bytes 98304 | tf_op jit(solution)/shard_map/all_to_all | solution.py:75
  210.5 36.4 %gather_fusion.1 = bf16[10240,128]{1,0:T(8,128)(2,1)} fusion(bf16[8192,128]{1,0:T(8,128)(2,1)S(1)} %copy-done, s32[10240]{0:T(1024)S(1)} %fusion.43), kind=kCustom, calls=%fused_computation.1 | custom fusion | bytes 5283840 | tf_op jit(solution)/shard_map/jit(_take)/gather | solution.py:64
  246.9 6.2 %select_select_fusion = bf16[32,320,128]{2,1,0:T(8,128)(2,1)} fusion(bf16[32,320,128]{2,1,0:T(8,128)(2,1)} %bitcast.91, pred[32,320]{1,0:T(8,128)(4,1)S(1)} %broadcast_in_dim.81, pred[32,320]{1,0:T(8,128)(4,1)S(1)} %broadcast_in_dim.79), kind=kLoop, calls=%fused_computation.18 | loop fusion | flops 2621440 | bytes 5263360 | tf_op jit(solution)/shard_map/jit(_where)/select_n | solution.py:63
  253.2 5.9 %all-to-all-start.1 = ((bf16[32,320,128]{2,1,0:T(8,128)(2,1)}), bf16[32,320,128]{2,1,0:T(8,128)(2,1)}, u32[]{:S(2)}, u32[]{:S(2)}) async-start(bf16[32,320,128]{2,1,0:T(8,128)(2,1)} %select_select_fusion), calls=%async_computation.1 | async-start | bytes 5242880 | tf_op jit(solution)/shard_map/all_to_all | solution.py:68
  259.2 59.2 %all-to-all-done.1 = bf16[32,320,128]{2,1,0:T(8,128)(2,1)} async-done(((bf16[32,320,128]{2,1,0:T(8,128)(2,1)}), bf16[32,320,128]{2,1,0:T(8,128)(2,1)}, u32[]{:S(2)}, u32[]{:S(2)}) %all-to-all-start.1) | async-done | bytes 2621472 | tf_op jit(solution)/shard_map/all_to_all | solution.py:68
  318.3 73.6 %while.26 = (s32[]{:T(128)}, bf16[16,256,128]{2,1,0:T(8,128)(2,1)S(1)}, s32[16]{0:T(128)S(1)}, bf16[10240,128]{1,0:T(8,128)(2,1)}, s32[10240]{0:T(1024)S(1)}, /*index=5*/s32[1]{0:T(128)}) while((s32[]{:T(128)}, bf16[16,256,128]{2,1,0:T(8,128)(2,1)S(1)}, s32[16]{0:T(128)S(1)}, bf16[10240,128]{1,0:T(8,128)(2,1)}, ...), condition=%wide.wide.region_6.7_spmd.clone.clone, body=%wide.wide.region_5.6_spmd.clone.sunk.clone | while | flops 673710336 | bytes 2795621 | solution.py:92
  319.6 3.3 fusion.87
  324.2 3.3 fusion.87
  328.8 3.3 fusion.87
  333.4 3.3 fusion.87
  338.0 3.3 fusion.87
  342.6 3.3 fusion.87
  347.2 3.3 fusion.87
  351.8 3.3 fusion.87
  356.4 3.3 fusion.87
  361.0 3.3 fusion.87
  365.6 3.3 fusion.87
  370.2 3.3 fusion.87
  374.8 3.3 fusion.87
  379.4 3.3 fusion.87
  384.0 3.3 fusion.87
  388.6 3.3 fusion.87
  392.0 1.9 collective-permute-start
  393.9 2.4 collective-permute-start.1
  396.8 3.6 collective-permute-done.1
  400.4 3.8 collective-permute-start.2
  406.5 2.1 collective-permute-done.3
  411.6 2.1 maximum_convert_fusion
  (400 shorter events, 151.8 us)
Async XLA Ops:
  0.6 209.9 %copy-start = (bf16[8192,128]{1,0:T(8,128)(2,1)S(1)}, bf16[8192,128]{1,0:T(8,128)(2,1)}, u32[]{:S(2)}) copy-start(bf16[8192,128]{1,0:T(8,128)(2,1)} %param.10) | copy-start | bytes 6291460
  7.9 137.7 %copy-start.1 = (s32[8192]{0:T(1024)S(1)}, s32[8192]{0:T(1024)}, u32[]{:S(2)}) copy-start(s32[8192]{0:T(1024)} %param.12) | copy-start | bytes 98308
  203.2 49.9 %all-to-all-start = ((s32[32,1,320]{2,1,0:T(1,128)}), s32[32,1,320]{2,1,0:T(1,128)S(1)}, u32[]{:S(2)}, u32[]{:S(2)}) async-start(s32[32,1,320]{2,1,0:T(1,128)} %all_to_all.11), calls=%async_computation | async-start | bytes 98304 | tf_op jit(solution)/shard_map/all_to_all | solution.py:75
  253.2 65.2 %all-to-all-start.1 = ((bf16[32,320,128]{2,1,0:T(8,128)(2,1)}), bf16[32,320,128]{2,1,0:T(8,128)(2,1)}, u32[]{:S(2)}, u32[]{:S(2)}) async-start(bf16[32,320,128]{2,1,0:T(8,128)(2,1)} %select_select_fusion), calls=%async_computation.1 | async-start | bytes 5242880 | tf_op jit(solution)/shard_map/all_to_all | solution.py:68
  318.3 78.0 %copy-start.3 = (bf16[3,3,128,128]{3,2,1,0:T(8,128)(2,1)S(1)}, bf16[3,3,128,128]{3,2,1,0:T(8,128)(2,1)}, u32[]{:S(2)}) copy-start(bf16[3,3,128,128]{3,2,1,0:T(8,128)(2,1)} %param.14) | copy-start | bytes 884740
  392.0 16.6 %copy-start.2 = (bf16[16,256,128]{2,1,0:T(8,128)(2,1)}, bf16[16,256,128]{2,1,0:T(8,128)(2,1)S(1)}, u32[]{:S(2)}) copy-start(bf16[16,256,128]{2,1,0:T(8,128)(2,1)S(1)} %get-tuple-element.67) | copy-start | bytes 3145732
  392.0 4.8 %collective-permute-start = (bf16[1,256,128]{2,1,0:T(8,128)(2,1)S(1)}, bf16[1,256,128]{2,1,0:T(8,128)(2,1)S(1)}, u32[]{:S(2)}, u32[]{:S(2)}) collective-permute-start(bf16[1,256,128]{2,1,0:T(8,128)(2,1)S(1)} %get-tuple-element.132), channel_id=1, source_target_pairs={{0,4},{4,8},{8,12},{12,16},{16,20},{20,24},{24,28},{1,5},{5,9},{9,... | collective-permute-start | bytes 196616 | tf_op jit(solution)/shard_map/ppermute | solution.py:18
  393.9 6.5 %collective-permute-start.1 = (bf16[1,256,128]{2,1,0:T(8,128)(2,1)S(1)}, bf16[1,256,128]{2,1,0:T(8,128)(2,1)S(1)}, u32[]{:S(2)}, u32[]{:S(2)}) collective-permute-start(bf16[1,256,128]{2,1,0:T(8,128)(2,1)S(1)} %get-tuple-element.133), channel_id=1, source_target_pairs={{4,0},{8,4},{12,8},{16,12},{20,16},{24,20},{28,24},{5,1},{9,5},{13... | collective-permute-start | bytes 196616 | tf_op jit(solution)/shard_map/ppermute | solution.py:20
  400.4 6.1 %collective-permute-start.2 = (bf16[18,1,128]{2,1,0:T(2,128)(2,1)S(1)}, bf16[18,1,128]{2,1,0:T(2,128)(2,1)S(1)}, u32[]{:S(2)}, u32[]{:S(2)}) collective-permute-start(bf16[18,1,128]{2,1,0:T(2,128)(2,1)S(1)} %get-tuple-element.131), channel_id=1, source_target_pairs={{0,1},{1,2},{2,3},{4,5},{5,6},{6,7},{8,9},{9,10},{10,11},{12,13},{... | collective-permute-start | bytes 13832 | tf_op jit(solution)/shard_map/ppermute | solution.py:18
  404.2 4.4 %collective-permute-start.3 = (bf16[18,1,128]{2,1,0:T(2,128)(2,1)S(1)}, bf16[18,1,128]{2,1,0:T(2,128)(2,1)S(1)}, u32[]{:S(2)}, u32[]{:S(2)}) collective-permute-start(bf16[18,1,128]{2,1,0:T(2,128)(2,1)S(1)} %get-tuple-element.130), channel_id=1, source_target_pairs={{1,0},{2,1},{3,2},{5,4},{6,5},{7,6},{9,8},{10,9},{11,10},{13,12},{... | collective-permute-start | bytes 13832 | tf_op jit(solution)/shard_map/ppermute | solution.py:20
  410.9 0.7 copy-start.4
where the time goes:
time: 415 us; the launch traced here: 414 us
  local copies, waits for them, and re-layouts  150 us (36%)
  other arithmetic  101 us (24%)
  waiting for transfers between devices  64.8 us (16%)
  matrix products  59.2 us (14%)
  starting transfers between devices  22.5 us (5%)
  loops' own time  13.9 us (3%)
    all_to_all x1, waiting for transfers between devices, shards(): lax.all_to_all(send_feats.reshape(devices, capacity, channels), ('gx', 'g...  59.2 us
    gather x1, local copies, waits for them, and re-layouts, shards(): send_cells = jnp.where(filled, jnp.take(point_cell, source_row, axis=0), -1)  56.8 us
    dot_general x16, matrix products, one_row(): return jnp.dot(onehot, got_feats, preferred_element_type=jnp.float32)  53.4 us
    reduce_sum x64, other arithmetic, pick(): return (found + jnp.sum(jnp.where(matches, owners, 0), axis=0), None)  48.8 us
    add x64, other arithmetic, pick(): owners = (first + inner_idx + 1)[:, None]  40.7 us
    dynamic_slice x64, local copies, waits for them, and re-layouts, shards(): lax.scan(pick, jnp.zeros((slots,), jnp.int32), (position.reshape(nblk, bl...  39.1 us
    gather x1, local copies, waits for them, and re-layouts, shards(): jnp.take(point_feats, source_row, axis=0)  36.4 us
    another operation x1, loops' own time, shards(): sums = lax.map(one_row, jnp.arange(ROWS_DEV, dtype=jnp.int32))  10.8 us
  transfers between devices with their start and end apart: 6, of which 3 were waited for; matrix products, arithmetic and copies ran while one was open for 11% of the time, Pallas kernels for 0%

commit v1 on v0

v1 whole, which is shorter than its diff:
```python
import functools

import jax
import jax.numpy as jnp
from jax import lax
from jax.experimental import pallas as pl
from jax.experimental.pallas import tpu as pltpu
from jax.sharding import PartitionSpec as P

COLS_DEV = 256
ROWS_DEV = 16
CELLS = ROWS_DEV * COLS_DEV


def with_halo(cells, sides, width):
    for axis, dim in sides:
        count = lax.axis_size(axis)
        ends = count - 1
        head = lax.slice_in_dim(cells, 0, width, axis=dim)
        tail = lax.slice_in_dim(cells, cells.shape[dim] - width, cells.shape[dim], axis=dim)
        cells = jnp.concatenate(
            [
                lax.ppermute(tail, axis, [(i, (i + 1) % count) for i in range(ends)]),
                cells,
                lax.ppermute(head, axis, [((i + 1) % count, i) for i in range(ends)]),
            ],
            axis=dim,
        )
    return cells


def pack_kernel(stride, words, counts, feats, out, cells, fbuf, obuf):
    points = feats.shape[0]
    devices, capacity, _ = out.shape
    step = 512

    @pl.loop(0, points // step)
    def _(i):
        rows = pl.ds(pl.multiple_of(i * step, step), step)
        fbuf[rows, :] = feats[rows, :].astype(jnp.float32)

    @pl.loop(0, points // 16)
    def _(i):
        base = i * 16
        for j in range(16):
            word = words[base + j]
            pos = lax.shift_right_logical(word, 12)
            cells[pos] = word & (CELLS - 1)
            obuf[pl.ds(pos, 1), :] = fbuf[pl.ds(base + j, 1), :]

    @pl.loop(0, devices)
    def _(t):
        cells[t * stride + capacity] = counts[t]
        rows = pl.ds(pl.multiple_of(t * stride, stride), capacity)
        out[t] = obuf[rows, :].astype(jnp.bfloat16)


def pack(words, counts, feats, capacity, stride):
    devices = counts.shape[0]
    points, channels = feats.shape
    smem = pl.BlockSpec(memory_space=pltpu.SMEM)
    vmem = pl.BlockSpec(memory_space=pltpu.VMEM)
    return pl.pallas_call(
        functools.partial(pack_kernel, stride),
        out_shape=(
            jax.ShapeDtypeStruct((devices, capacity, channels), jnp.bfloat16),
            jax.ShapeDtypeStruct(((devices + 1) * stride,), jnp.int32),
        ),
        in_specs=[smem, smem, vmem],
        out_specs=(vmem, smem),
        scratch_shapes=[
            pltpu.VMEM((points, channels), jnp.float32),
            pltpu.VMEM((devices * stride + 8, channels), jnp.float32),
        ],
        compiler_params=pltpu.CompilerParams(vmem_limit_bytes=48 * 1024 * 1024),
        name="pack",
    )(words, counts, feats)


def scatter_kernel(feats, rows, cols, out, acc):
    step = pl.program_id(0)
    chunk = feats.shape[0]

    @pl.when(step == 0)
    def _():
        acc[...] = jnp.zeros_like(acc)

    ids = lax.broadcasted_iota(jnp.int32, (COLS_DEV, chunk), 0)
    onehot = jnp.where(ids == cols[0], 1.0, 0.0).astype(jnp.bfloat16)
    values = feats[...]
    row = rows[...]
    zero = jnp.zeros_like(values)
    for r in range(0, ROWS_DEV, 2):
        masked = jnp.concatenate(
            [jnp.where(row == jnp.bfloat16(r + k), values, zero) for k in range(2)], axis=1
        )
        part = jnp.dot(onehot, masked, preferred_element_type=jnp.float32)
        acc[:, r * 128 : (r + 2) * 128] += part

    @pl.when(step == pl.num_programs(0) - 1)
    def _():
        for r in range(ROWS_DEV):
            out[r] = acc[:, r * 128 : (r + 1) * 128].astype(jnp.bfloat16)


def scatter(feats, rows, cols, chunk):
    total, channels = feats.shape
    return pl.pallas_call(
        scatter_kernel,
        grid=(total // chunk,),
        out_shape=jax.ShapeDtypeStruct((ROWS_DEV, COLS_DEV, channels), jnp.bfloat16),
        in_specs=[
            pl.BlockSpec((chunk, channels), lambda i: (i, 0)),
            pl.BlockSpec((chunk, channels), lambda i: (i, 0)),
            pl.BlockSpec((1, 1, chunk), lambda i: (i, 0, 0)),
        ],
        out_specs=pl.BlockSpec((ROWS_DEV, COLS_DEV, channels), lambda i: (0, 0, 0)),
        scratch_shapes=[pltpu.VMEM((COLS_DEV, ROWS_DEV * channels), jnp.float32)],
        compiler_params=pltpu.CompilerParams(vmem_limit_bytes=48 * 1024 * 1024),
        name="scatter",
    )(feats, rows, cols.reshape(total // chunk, 1, chunk))


def places(target, live, devices):
    points = target.shape[0]
    blk = 256
    nblk = points // blk
    tile_ids = jnp.arange(devices, dtype=jnp.int32)
    hits = (tile_ids[:, None] == target[None, :]) & live[None, :]
    inner_idx = jnp.arange(blk, dtype=jnp.int32)
    upper = (inner_idx[:, None] <= inner_idx[None, :]).astype(jnp.bfloat16)
    blocks = hits.astype(jnp.bfloat16).reshape(devices, nblk, blk)
    inner = jnp.einsum("dbj,ji->dbi", blocks, upper, preferred_element_type=jnp.float32)
    totals = inner[:, :, -1]
    running = jnp.cumsum(totals, axis=1)
    ranks = inner + (running - totals)[:, :, None]
    place = jnp.sum(jnp.where(hits.reshape(devices, nblk, blk), ranks, 0.0), axis=0)
    return place.reshape(points).astype(jnp.int32) - 1, running[:, -1].astype(jnp.int32)


def shards(point_feats, point_tile, point_cell, point_count, conv_weight, conv_bias):
    size_gx = lax.axis_size("gx")
    size_gy = lax.axis_size("gy")
    devices = size_gx * size_gy
    points = point_feats.shape[0]
    channels = point_feats.shape[1]
    capacity = 5 * points // (4 * devices)
    stride = -(-(capacity + 1) // 128) * 128
    target = point_tile[:, 0]
    live = jnp.arange(points, dtype=jnp.int32) < point_count[0]
    place, counts = places(target, live, devices)
    position = jnp.where(live, target * stride + place, devices * stride)
    words = position * CELLS + point_cell
    send_feats, send_cells = pack(words, counts, point_feats, capacity, stride)
    got_cells = lax.all_to_all(
        send_cells[: devices * stride].reshape(devices, stride),
        ("gx", "gy"),
        split_axis=0,
        concat_axis=0,
        tiled=True,
    )
    got_feats = lax.all_to_all(
        send_feats, ("gx", "gy"), split_axis=0, concat_axis=0, tiled=True
    ).reshape(-1, channels)
    filled = jnp.arange(capacity, dtype=jnp.int32)[None, :] < got_cells[:, capacity : capacity + 1]
    cells = got_cells[:, :capacity]
    rows = jnp.where(filled, cells // COLS_DEV, -1).reshape(-1)
    cols = jnp.where(filled, cells % COLS_DEV, 0).reshape(-1)
    rows = jnp.broadcast_to(rows.astype(jnp.bfloat16)[:, None], got_feats.shape)
    bev_map = scatter(got_feats, rows, cols, devices * capacity // 8)
    padded = with_halo(bev_map, (("gx", 0), ("gy", 1)), 1)
    total = jnp.zeros((ROWS_DEV, COLS_DEV, channels), jnp.float32)
    for shift_row in range(3):
        for shift_col in range(3):
            window = padded[shift_row : shift_row + ROWS_DEV, shift_col : shift_col + COLS_DEV]
            total = total + jnp.einsum(
                "rcd,de->rce",
                window,
                conv_weight[shift_row, shift_col],
                preferred_element_type=jnp.float32,
            )
    conv_out = jax.nn.relu(total + conv_bias).astype(jnp.bfloat16)
    return (bev_map, conv_out)


def solution(mesh):
    in_specs = (
        P(("gx", "gy"), None),
        P(("gx", "gy"), None),
        P(("gx", "gy")),
        P(("gx", "gy")),
        P(),
        P(),
    )
    out_specs = (P("gx", "gy", None), P("gx", "gy", None))
    return jax.shard_map(shards, mesh=mesh, in_specs=in_specs, out_specs=out_specs, check_vma=False)
```

time: 415 us -> 149 us (0.36)
  local copies, waits for them, and re-layouts: 150 us -> 10 us
  other arithmetic: 101 us -> 4.41 us
  matrix products: 59.2 us -> 7.26 us
  Pallas kernels: 0 us -> 35.4 us
  loops' own time: 13.9 us -> 0 us
  blocking collectives: 0 us -> 13.7 us
  starting transfers between devices: 22.5 us -> 12.6 us
    gather x2 -> x0, local copies, waits for them, and re-layouts: 93.2 us -> none  [the longest x1 56.8 us: shards(): send_cells = jnp.where(filled, jnp.take(point_cell, source_row, axis=0), -1)]
    dot_general x17 -> x1, matrix products: 53.7 us -> 0.33 us  [places(): jnp.einsum('dbj,ji->dbi', blocks, upper, preferred_element_type=jnp.float32)]
    reduce_sum x65 -> x1, other arithmetic: 51.5 us -> 0.27 us  [places(): jnp.sum(jnp.where(hits.reshape(devices, nblk, blk), ranks, 0.0), axis=0)]
    dynamic_slice x80 -> x0, local copies, waits for them, and re-layouts: 48.5 us -> none  [the longest x64 39.1 us: shards(): lax.scan(pick, jnp.zeros((slots,), jnp.int32), (position.reshape(nblk, bl...]
    add x145 -> x1, other arithmetic: 42.2 us -> 0.01 us  [shards(): words = position * CELLS + point_cell]
    pallas_call x0 -> x2, Pallas kernels: none -> 35.4 us  [the longest x1 21 us: pack(): pl.pallas_call(functools.partial(pack_kernel, stride), out_shape=(jax.Sha...]
    another operation x2 -> x0, loops' own time: 13.9 us -> none  [the longest x1 10.8 us: shards(): sums = lax.map(one_row, jnp.arange(ROWS_DEV, dtype=jnp.int32))]
    all_to_all x0 -> x1, blocking collectives: none -> 13.7 us  [shards(): lax.all_to_all(send_cells[:devices * stride].reshape(devices, stride), ('...]
  transfers between devices with their start and end apart: 6 -> 5, of which waited for: 3 -> 3; matrix products, arithmetic and copies ran while one was open for 11% -> 2% of each run, Pallas kernels for 0% -> 0%
where the time goes in v1:
time: 149 us; the launch traced here: 148 us
  waiting for transfers between devices  63.5 us (43%)
  Pallas kernels  35.4 us (24%)
  blocking collectives  13.7 us (9%)
  starting transfers between devices  12.6 us (8%)
  local copies, waits for them, and re-layouts  10 us (7%)
  matrix products  7.26 us (5%)
  other arithmetic  4.41 us (3%)
  between operations  1.53 us (1%)
    all_to_all x1, waiting for transfers between devices, shards(): lax.all_to_all(send_feats, ('gx', 'gy'), split_axis=0, concat_axis=0, til...  58.8 us
    pallas_call x1, Pallas kernels, pack(): pl.pallas_call(functools.partial(pack_kernel, stride), out_shape=(jax.Sha...  21 us
    pallas_call x1, Pallas kernels, scatter(): pl.pallas_call(scatter_kernel, grid=(total // chunk,), out_shape=jax.Shap...  14.4 us
    all_to_all x1, blocking collectives, shards(): lax.all_to_all(send_cells[:devices * stride].reshape(devices, stride), ('...  13.7 us
    dot_general x9, matrix products, shards(): jnp.einsum('rcd,de->rce', window, conv_weight[shift_row, shift_col], pref...  6.93 us
    ppermute x2, starting transfers between devices, with_halo(): lax.ppermute(tail, axis, [(i, (i + 1) % count) for i in range(ends)])  5.71 us
    broadcast_in_dim x1, local copies, waits for them, and re-layouts, shards(): rows = jnp.broadcast_to(rows.astype(jnp.bfloat16)[:, None], got_feats.shape)  4.91 us
    ppermute x2, waiting for transfers between devices, with_halo(): lax.ppermute(head, axis, [((i + 1) % count, i) for i in range(ends)])  4.68 us
  transfers between devices with their start and end apart: 5, of which 3 were waited for; matrix products, arithmetic and copies ran while one was open for 2% of the time, Pallas kernels for 0%

profile of v1, /device:TPU:1, one launch (start us, length us, event | category | flops | bytes accessed | tf_op | source)
XLA Modules:
  0.0 148.4 jit_solution(3292119628237550817)
XLA Ops:
  0.6 0.5 broadcast.53
  1.1 1.5 %fusion.57 = (s32[8192]{0:T(1024)S(1)}, s32[8192,1]{0,1:T(1,128)S(1)}) fusion(s32[8192,1]{0,1:T(1,128)} %param.7, s32[]{:T(128)} %broadcast.53), kind=kLoop, calls=%fused_computation.80 | loop fusion | flops 8192 | bytes 98308 | tf_op args[1]
  3.4 0.3 fusion.23
  3.7 0.4 slice_reduce_fusion
  4.4 1.1 copy.11
  5.5 1.4 subtract_reduce_fusion
  6.9 0.3 select_reduce_fusion
  7.3 21.0 %pack.1 = (bf16[32,320,128]{2,1,0:T(8,128)(2,1)S(1)}, s32[12672]{0:T(1024)S(1)}) custom-call(s32[8192]{0:T(1024)S(1)} %multiply_add_fusion.words, s32[32]{0:T(128)S(1)} %fusion.53.counts, bf16[8192,128]{1,0:T(8,128)(2,1)S(1)} %copy-done.1), custom_call_target="tpu_custom_call" | custom-call | tf_op jit(solution)/shard_map/pack/pallas_call | solution.py:63
  28.3 1.5 %copy-done = bf16[32,320,128]{2,1,0:T(8,128)(2,1)} copy-done((bf16[32,320,128]{2,1,0:T(8,128)(2,1)}, bf16[32,320,128]{2,1,0:T(8,128)(2,1)S(1)}, u32[]{:S(2)}) %copy-start) | copy-done | bytes 2621464
  29.8 13.7 %all_to_all.14 = s32[32,1,384]{2,1,0:T(1,128)S(1)} all-to-all(s32[32,1,384]{2,1,0:T(1,128)S(1)} %bitcast.67), channel_id=1, replica_groups=mesh['gx'=8,'gy'=4] {'gx','gy'}, dimensions={0} | all-to-all | bytes 98304 | tf_op jit(solution)/shard_map/all_to_all | solution.py:155
  43.5 3.2 %all-to-all-start = ((bf16[32,320,128]{2,1,0:T(8,128)(2,1)}), bf16[32,320,128]{2,1,0:T(8,128)(2,1)S(1)}, u32[]{:S(2)}, u32[]{:S(2)}) async-start(bf16[32,320,128]{2,1,0:T(8,128)(2,1)} %copy-done), calls=%async_computation | async-start | bytes 5242880 | tf_op jit(solution)/shard_map/all_to_all | solution.py:162
  47.3 58.8 %all-to-all-done = bf16[32,320,128]{2,1,0:T(8,128)(2,1)S(1)} async-done(((bf16[32,320,128]{2,1,0:T(8,128)(2,1)}), bf16[32,320,128]{2,1,0:T(8,128)(2,1)S(1)}, u32[]{:S(2)}, u32[]{:S(2)}) %all-to-all-start) | async-done | bytes 2621472 | tf_op jit(solution)/shard_map/all_to_all | solution.py:162
  106.1 4.9 %broadcast_in_dim.15.rows = bf16[10240,128]{1,0:T(8,128)(2,1)S(1)} broadcast(bf16[10240]{0:T(1024)(128)(2,1)S(1)} %convert_element_type.28), dimensions={0} | broadcast | bytes 2641920 | tf_op jit(solution)/shard_map/broadcast_in_dim | solution.py:169
  111.0 14.4 %scatter.1 = bf16[16,256,128]{2,1,0:T(8,128)(2,1)} custom-call(bf16[10240,128]{1,0:T(8,128)(2,1)S(1)} %bitcast.63, bf16[10240,128]{1,0:T(8,128)(2,1)S(1)} %broadcast_in_dim.15.rows, s32[8,1,1280]{2,1,0:T(1,128)S(1)} %reshape_reshape.3.cols), custom_call_target="tpu_custom_call" | custom-call | tf_op jit(solution)/shard_map/scatter/pallas_call | solution.py:108
  125.4 1.0 fusion.56
  126.4 1.9 %collective-permute-start = (bf16[1,256,128]{2,1,0:T(8,128)(2,1)S(1)}, bf16[1,256,128]{2,1,0:T(8,128)(2,1)S(1)}, u32[]{:S(2)}, u32[]{:S(2)}) collective-permute-start(bf16[1,256,128]{2,1,0:T(8,128)(2,1)S(1)} %get-tuple-element.12), channel_id=1, source_target_pairs={{0,4},{4,8},{8,12},{12,16},{16,20},{20,24},{24,28},{1,5},{5,9},{9,... | collective-permute-start | bytes 196616 | tf_op jit(solution)/shard_map/ppermute | solution.py:23
  128.3 2.4 %collective-permute-start.1 = (bf16[1,256,128]{2,1,0:T(8,128)(2,1)S(1)}, bf16[1,256,128]{2,1,0:T(8,128)(2,1)S(1)}, u32[]{:S(2)}, u32[]{:S(2)}) collective-permute-start(bf16[1,256,128]{2,1,0:T(8,128)(2,1)S(1)} %get-tuple-element.13), channel_id=1, source_target_pairs={{4,0},{8,4},{12,8},{16,12},{20,16},{24,20},{28,24},{5,1},{9,5},{13... | collective-permute-start | bytes 196616 | tf_op jit(solution)/shard_map/ppermute | solution.py:25
  130.7 1.6 %fusion.37 = f32[16,256,128]{2,1,0:T(8,128)S(1)} fusion(bf16[16,256,128]{2,1,0:T(8,128)(2,1)} %scatter.1, bf16[3,3,128,128]{3,2,1,0:T(8,128)(2,1)S(1)} %copy-done.3), kind=kOutput, calls=%fused_computation.50 | convolution fusion | flops 134217728 | bytes 3178496 | tf_op jit(solution)/shard_map/rcd,de->rce/dot_general | solution.py:176
  132.4 2.4 %collective-permute-done.1 = bf16[1,256,128]{2,1,0:T(8,128)(2,1)S(1)} collective-permute-done((bf16[1,256,128]{2,1,0:T(8,128)(2,1)S(1)}, bf16[1,256,128]{2,1,0:T(8,128)(2,1)S(1)}, u32[]{:S(2)}, u32[]{:S(2)}) %collective-permute-start.1) | collective-permute-done | bytes 65568 | tf_op jit(solution)/shard_map/ppermute | solution.py:25
  134.8 3.8 %collective-permute-start.2 = (bf16[18,1,128]{2,1,0:T(2,128)(2,1)S(1)}, bf16[18,1,128]{2,1,0:T(2,128)(2,1)S(1)}, u32[]{:S(2)}, u32[]{:S(2)}) collective-permute-start(bf16[18,1,128]{2,1,0:T(2,128)(2,1)S(1)} %get-tuple-element.11), channel_id=1, source_target_pairs={{0,1},{1,2},{2,3},{4,5},{5,6},{6,7},{8,9},{9,10},{10,11},{12,13},{... | collective-permute-start | bytes 13832 | tf_op jit(solution)/shard_map/ppermute | solution.py:23
  138.6 1.3 collective-permute-start.3
  139.9 0.4 fusion
  140.3 0.4 fusion.4
  140.8 2.3 %collective-permute-done.3 = bf16[18,1,128]{2,1,0:T(2,128)(2,1)S(1)} collective-permute-done((bf16[18,1,128]{2,1,0:T(2,128)(2,1)S(1)}, bf16[18,1,128]{2,1,0:T(2,128)(2,1)S(1)}, u32[]{:S(2)}, u32[]{:S(2)}) %collective-permute-start.3) | collective-permute-done | bytes 4640 | tf_op jit(solution)/shard_map/ppermute | solution.py:25
  143.0 0.6 pad_maximum_fusion
  143.7 0.4 fusion.12
  144.1 0.4 fusion.16
  144.5 0.4 fusion.14
  145.0 0.4 fusion.18
  145.4 0.4 fusion.20
  145.8 0.2 copy-done.5
  146.0 2.4 %maximum_convert_fusion = bf16[16,256,128]{2,1,0:T(8,128)(2,1)} fusion(f32[16,256,128]{2,1,0:T(8,128)S(1)} %fusion.4, f32[16,256,128]{2,1,0:T(8,128)S(1)} %fusion.12, f32[16,256,128]{2,1,0:T(8,128)S(1)} %fusion.14, f32[16,256,128]{2,1,0:T(8,128)S(1)} %fusion.37, f32[16,256,128]{2,1,0:T(8,128)S(1)} %fusion.16, f32[16,256,128]{2,1,0:T(8,128)S(1)} %fusion.18, ...), kind=kOutput, calls=%fused_computation | convolution fusion | flops 139984896 | bytes 18907648 | tf_op jit(solution)/shard_map/rcd,de->rce/dot_general | solution.py:176
  (27 shorter events, 1.0 us)
Async XLA Ops:
  3.3 3.9 %copy-start.4 = (s32[8192]{0:T(1024)S(1)}, s32[8192]{0:T(1024)}, u32[]{:S(2)}) copy-start(s32[8192]{0:T(1024)} %param.8) | copy-start | bytes 98308
  3.3 4.0 %copy-start.1 = (bf16[8192,128]{1,0:T(8,128)(2,1)S(1)}, bf16[8192,128]{1,0:T(8,128)(2,1)}, u32[]{:S(2)}) copy-start(bf16[8192,128]{1,0:T(8,128)(2,1)} %feats.1) | copy-start | bytes 6291460
  28.3 1.5 %copy-start = (bf16[32,320,128]{2,1,0:T(8,128)(2,1)}, bf16[32,320,128]{2,1,0:T(8,128)(2,1)S(1)}, u32[]{:S(2)}) copy-start(bf16[32,320,128]{2,1,0:T(8,128)(2,1)S(1)} %get-tuple-element.4) | copy-start | bytes 7864324
  43.5 62.6 %all-to-all-start = ((bf16[32,320,128]{2,1,0:T(8,128)(2,1)}), bf16[32,320,128]{2,1,0:T(8,128)(2,1)S(1)}, u32[]{:S(2)}, u32[]{:S(2)}) async-start(bf16[32,320,128]{2,1,0:T(8,128)(2,1)} %copy-done), calls=%async_computation | async-start | bytes 5242880 | tf_op jit(solution)/shard_map/all_to_all | solution.py:162
  111.0 19.8 %copy-start.3 = (bf16[3,3,128,128]{3,2,1,0:T(8,128)(2,1)S(1)}, bf16[3,3,128,128]{3,2,1,0:T(8,128)(2,1)}, u32[]{:S(2)}) copy-start(bf16[3,3,128,128]{3,2,1,0:T(8,128)(2,1)} %param.10) | copy-start | bytes 884740
  125.4 9.4 %copy-start.2 = (bf16[16,256,128]{2,1,0:T(8,128)(2,1)S(1)}, bf16[16,256,128]{2,1,0:T(8,128)(2,1)}, u32[]{:S(2)}) copy-start(bf16[16,256,128]{2,1,0:T(8,128)(2,1)} %scatter.1) | copy-start | bytes 3145732
  126.4 6.0 %collective-permute-start = (bf16[1,256,128]{2,1,0:T(8,128)(2,1)S(1)}, bf16[1,256,128]{2,1,0:T(8,128)(2,1)S(1)}, u32[]{:S(2)}, u32[]{:S(2)}) collective-permute-start(bf16[1,256,128]{2,1,0:T(8,128)(2,1)S(1)} %get-tuple-element.12), channel_id=1, source_target_pairs={{0,4},{4,8},{8,12},{12,16},{16,20},{20,24},{24,28},{1,5},{5,9},{9,... | collective-permute-start | bytes 196616 | tf_op jit(solution)/shard_map/ppermute | solution.py:23
  128.3 6.5 %collective-permute-start.1 = (bf16[1,256,128]{2,1,0:T(8,128)(2,1)S(1)}, bf16[1,256,128]{2,1,0:T(8,128)(2,1)S(1)}, u32[]{:S(2)}, u32[]{:S(2)}) collective-permute-start(bf16[1,256,128]{2,1,0:T(8,128)(2,1)S(1)} %get-tuple-element.13), channel_id=1, source_target_pairs={{4,0},{8,4},{12,8},{16,12},{20,16},{24,20},{28,24},{5,1},{9,5},{13... | collective-permute-start | bytes 196616 | tf_op jit(solution)/shard_map/ppermute | solution.py:25
  134.8 5.9 %collective-permute-start.2 = (bf16[18,1,128]{2,1,0:T(2,128)(2,1)S(1)}, bf16[18,1,128]{2,1,0:T(2,128)(2,1)S(1)}, u32[]{:S(2)}, u32[]{:S(2)}) collective-permute-start(bf16[18,1,128]{2,1,0:T(2,128)(2,1)S(1)} %get-tuple-element.11), channel_id=1, source_target_pairs={{0,1},{1,2},{2,3},{4,5},{5,6},{6,7},{8,9},{9,10},{10,11},{12,13},{... | collective-permute-start | bytes 13832 | tf_op jit(solution)/shard_map/ppermute | solution.py:23
  138.6 4.4 %collective-permute-start.3 = (bf16[18,1,128]{2,1,0:T(2,128)(2,1)S(1)}, bf16[18,1,128]{2,1,0:T(2,128)(2,1)S(1)}, u32[]{:S(2)}, u32[]{:S(2)}) collective-permute-start(bf16[18,1,128]{2,1,0:T(2,128)(2,1)S(1)} %get-tuple-element.10), channel_id=1, source_target_pairs={{1,0},{2,1},{3,2},{5,4},{6,5},{7,6},{9,8},{10,9},{11,10},{13,12},{... | collective-permute-start | bytes 13832 | tf_op jit(solution)/shard_map/ppermute | solution.py:25
  145.4 0.7 copy-start.5

commit v2 on v1

v2 whole, which is shorter than its diff:
```python
import functools

import jax
import jax.numpy as jnp
from jax import lax
from jax.experimental import pallas as pl
from jax.experimental.pallas import tpu as pltpu
from jax.sharding import PartitionSpec as P

COLS_DEV = 256
ROWS_DEV = 16
CELLS = ROWS_DEV * COLS_DEV


def pack_kernel(stride, words, feats, out, cells, fbuf, obuf):
    points = feats.shape[0]
    devices, capacity, _ = out.shape
    step = 512

    @pl.loop(0, points // step)
    def _(i):
        rows = pl.ds(pl.multiple_of(i * step, step), step)
        fbuf[rows, :] = feats[rows, :].astype(jnp.float32)

    @pl.loop(0, points // 16)
    def _(i):
        base = i * 16
        for j in range(16):
            word = words[base + j]
            pos = lax.shift_right_logical(word, 12)
            cells[pos] = word & (CELLS - 1)
            obuf[pl.ds(pos, 1), :] = fbuf[pl.ds(base + j, 1), :]

    @pl.loop(0, devices)
    def _(t):
        rows = pl.ds(pl.multiple_of(t * stride, stride), capacity)
        out[t] = obuf[rows, :].astype(jnp.bfloat16)


def pack(words, feats, devices, capacity, stride):
    points, channels = feats.shape
    smem = pl.BlockSpec(memory_space=pltpu.SMEM)
    vmem = pl.BlockSpec(memory_space=pltpu.VMEM)
    return pl.pallas_call(
        functools.partial(pack_kernel, stride),
        out_shape=(
            jax.ShapeDtypeStruct((devices, capacity, channels), jnp.bfloat16),
            jax.ShapeDtypeStruct(((devices + 1) * stride,), jnp.int32),
        ),
        in_specs=[smem, vmem],
        out_specs=(vmem, smem),
        scratch_shapes=[
            pltpu.VMEM((points, channels), jnp.float32),
            pltpu.VMEM((devices * stride + 8, channels), jnp.float32),
        ],
        compiler_params=pltpu.CompilerParams(vmem_limit_bytes=48 * 1024 * 1024),
        name="pack",
    )(words, feats)


MESH = pl.DeviceIdType.MESH
GROUP = 4
NEIGHBOURS = [(dx, dy) for dx in (-1, 0, 1) for dy in (-1, 0, 1) if (dx, dy) != (0, 0)]


def map_kernel(
    size_gx,
    size_gy,
    send_feats,
    send_cells,
    weight,
    bias,
    bev,
    conv,
    got_feats,
    got_cells,
    acc,
    pad,
    edges,
    sides,
    flat,
    send_f,
    recv_f,
    send_c,
    recv_c,
    own,
    send_h,
    recv_h,
):
    devices = size_gx * size_gy
    capacity = send_feats.shape[1]
    gx, gy = lax.axis_index("gx"), lax.axis_index("gy")
    me = gx * size_gy + gy

    for r in (0, ROWS_DEV + 1):
        pad[r] = jnp.zeros_like(pad[r])
    sides[...] = jnp.zeros_like(sides)

    barrier = pltpu.get_barrier_semaphore()

    @pl.loop(1, devices)
    def _(k):
        other = lax.rem(me + k, devices)
        pl.semaphore_signal(
            barrier, inc=1, device_id=(other // size_gy, lax.rem(other, size_gy)), device_id_type=MESH
        )

    pl.semaphore_wait(barrier, devices - 1)

    def copies(source, owner, target):
        where = dict(
            device_id=(target // size_gy, lax.rem(target, size_gy)), device_id_type=MESH
        )
        return (
            pltpu.make_async_remote_copy(
                send_cells.at[source], got_cells.at[owner],
                send_c.at[source], recv_c.at[owner], **where,
            ),
            pltpu.make_async_remote_copy(
                send_feats.at[source], got_feats.at[owner, pl.ds(0, capacity)],
                send_f.at[source], recv_f.at[owner], **where,
            ),
        )

    @pl.loop(1, devices)
    def _(k):
        other = lax.rem(me + k, devices)
        for copy in copies(other, me, other):
            copy.start()

    mine = (
        pltpu.make_async_copy(send_cells.at[me], got_cells.at[me], own.at[0]),
        pltpu.make_async_copy(
            send_feats.at[me], got_feats.at[me, pl.ds(0, capacity)], own.at[1]
        ),
    )
    for copy in mine:
        copy.start()
    acc[...] = jnp.zeros_like(acc)
    for copy in mine:
        copy.wait()

    @pl.loop(0, devices // GROUP)
    def _(g):
        owners = [lax.rem(me + devices - (g * GROUP + j), devices) for j in range(GROUP)]
        for j, owner in enumerate(owners):

            @pl.when(g * GROUP + j > 0)
            def _():
                for copy in copies(owner, owner, owner):
                    copy.wait_recv()

        cells = jnp.concatenate([got_cells[owner] for owner in owners], axis=1)
        values = jnp.concatenate([got_feats[owner] for owner in owners], axis=0)
        length = cells.shape[1]
        row = jnp.right_shift(cells, 8).astype(jnp.float32)
        row = jnp.transpose(jnp.broadcast_to(row, (128, length))).astype(jnp.bfloat16)
        col = cells & (COLS_DEV - 1)
        ids = lax.broadcasted_iota(jnp.int32, (COLS_DEV, length), 0)
        onehot = jnp.where(ids == col, 1.0, 0.0).astype(jnp.bfloat16)
        zero = jnp.zeros_like(values)
        for r in range(0, ROWS_DEV, 2):
            masked = jnp.concatenate(
                [jnp.where(row == jnp.bfloat16(r + k), values, zero) for k in range(2)], axis=1
            )
            part = jnp.dot(onehot, masked, preferred_element_type=jnp.float32)
            acc[:, r * 128 : (r + 2) * 128] += part

    for r in range(ROWS_DEV):
        for side, c in ((0, 0), (1, COLS_DEV - 1)):
            edge = acc[c : c + 1, r * 128 : (r + 1) * 128]
            edges[side, r] = edge.astype(jnp.bfloat16).astype(jnp.float32)
    for r in range(ROWS_DEV):
        cells = acc[:, r * 128 : (r + 1) * 128].astype(jnp.bfloat16)
        pad[r + 1] = cells
        bev[r] = cells

    def inside(x, y):
        return (x >= 0) & (x < size_gx) & (y >= 0) & (y < size_gy)

    def halo(i):
        dx, dy = NEIGHBOURS[i]
        if dy == 0:
            src, dst = (pad.at[1], pad.at[ROWS_DEV + 1]) if dx < 0 else (pad.at[ROWS_DEV], pad.at[0])
        else:
            from_side, to_side = (0, 1) if dy < 0 else (1, 0)
            if dx == 0:
                src = edges.at[from_side]
                dst = sides.at[to_side, pl.ds(1, ROWS_DEV)]
            else:
                at = 0 if dx < 0 else ROWS_DEV - 1
                src = edges.at[from_side, pl.ds(at, 1)]
                dst = sides.at[to_side, pl.ds(ROWS_DEV + 1 if dx < 0 else 0, 1)]
        return pltpu.make_async_remote_copy(
            src, dst, send_h.at[i], recv_h.at[i], device_id=(gx + dx, gy + dy), device_id_type=MESH
        )

    for i, (dx, dy) in enumerate(NEIGHBOURS):

        @pl.when(inside(gx + dx, gy + dy))
        def _():
            halo(i).start()

    for i, (dx, dy) in enumerate(NEIGHBOURS):

        @pl.when(inside(gx - dx, gy - dy))
        def _():
            halo(i).wait_recv()

    side_sums = []
    for side in range(2):
        for r in range(ROWS_DEV + 2):
            flat[r : r + 1, :] = sides[side, r]
        near = jnp.concatenate([flat[a : a + ROWS_DEV, :] for a in range(3)], axis=1)
        taps = weight[:, :128] if side == 0 else weight[:, 256:]
        side_sums.append(
            jnp.dot(near.astype(jnp.bfloat16), taps, preferred_element_type=jnp.float32)
        )
    for side in range(2):
        flat[side * ROWS_DEV : (side + 1) * ROWS_DEV, :] = side_sums[side]
    place = lax.broadcasted_iota(jnp.int32, (COLS_DEV, 128), 0)

    @pl.loop(0, ROWS_DEV)
    def _(r):
        near = jnp.concatenate([pad[r + a] for a in range(3)], axis=1)
        sums = jnp.dot(near, weight[...], preferred_element_type=jnp.float32)
        left = jnp.where(place == 0, flat[pl.ds(r, 1), :], pltpu.roll(sums[:, :128], 1, 0))
        right = jnp.where(
            place == COLS_DEV - 1,
            flat[pl.ds(r + ROWS_DEV, 1), :],
            pltpu.roll(sums[:, 256:], COLS_DEV - 1, 0),
        )
        total = sums[:, 128:256] + left + right + bias[...]
        conv[r] = jnp.maximum(total, 0.0).astype(jnp.bfloat16)

    for i, (dx, dy) in enumerate(NEIGHBOURS):

        @pl.when(inside(gx + dx, gy + dy))
        def _():
            halo(i).wait_send()

    @pl.loop(1, devices)
    def _(k):
        other = lax.rem(me + k, devices)
        for copy in copies(other, me, other):
            copy.wait_send()


def make_map(feats, cells, weight, bias, size_gx, size_gy):
    devices, capacity, channels = feats.shape
    stride = cells.shape[-1]
    vmem = pl.BlockSpec(memory_space=pltpu.VMEM)
    shape = jax.ShapeDtypeStruct((ROWS_DEV, COLS_DEV, channels), jnp.bfloat16)
    dma = pltpu.SemaphoreType.DMA
    return pl.pallas_call(
        functools.partial(map_kernel, size_gx, size_gy),
        out_shape=(shape, shape),
        in_specs=[vmem] * 4,
        out_specs=(vmem, vmem),
        scratch_shapes=[
            pltpu.VMEM((devices, stride, channels), jnp.bfloat16),
            pltpu.VMEM((devices, 1, stride), jnp.int32),
            pltpu.VMEM((COLS_DEV, ROWS_DEV * channels), jnp.float32),
            pltpu.VMEM((ROWS_DEV + 2, COLS_DEV, channels), jnp.bfloat16),
            pltpu.VMEM((2, ROWS_DEV, 1, channels), jnp.float32),
            pltpu.VMEM((2, ROWS_DEV + 2, 1, channels), jnp.float32),
            pltpu.VMEM((2 * ROWS_DEV, channels), jnp.float32),
            dma((devices,)),
            dma((devices,)),
            dma((devices,)),
            dma((devices,)),
            dma((2,)),
            dma((len(NEIGHBOURS),)),
            dma((len(NEIGHBOURS),)),
        ],
        compiler_params=pltpu.CompilerParams(
            collective_id=0, has_side_effects=True, vmem_limit_bytes=56 * 1024 * 1024
        ),
        name="make_map",
    )(feats, cells, weight, bias)


def places(target, live, devices):
    points = target.shape[0]
    blk = 256
    nblk = points // blk
    tile_ids = jnp.arange(devices, dtype=jnp.int32)
    hits = (tile_ids[:, None] == target[None, :]) & live[None, :]
    inner_idx = jnp.arange(blk, dtype=jnp.int32)
    upper = (inner_idx[:, None] <= inner_idx[None, :]).astype(jnp.bfloat16)
    blocks = hits.astype(jnp.bfloat16).reshape(devices, nblk, blk)
    inner = jnp.einsum("dbj,ji->dbi", blocks, upper, preferred_element_type=jnp.float32)
    totals = inner[:, :, -1]
    running = jnp.cumsum(totals, axis=1)
    ranks = inner + (running - totals)[:, :, None]
    place = jnp.sum(jnp.where(hits.reshape(devices, nblk, blk), ranks, 0.0), axis=0)
    return place.reshape(points).astype(jnp.int32) - 1, running[:, -1].astype(jnp.int32)


def shards(point_feats, point_tile, point_cell, point_count, conv_weight, conv_bias):
    size_gx = lax.axis_size("gx")
    size_gy = lax.axis_size("gy")
    devices = size_gx * size_gy
    points = point_feats.shape[0]
    channels = point_feats.shape[1]
    capacity = 5 * points // (4 * devices)
    stride = -(-capacity // 128) * 128
    target = point_tile[:, 0]
    live = jnp.arange(points, dtype=jnp.int32) < point_count[0]
    place, counts = places(target, live, devices)
    position = jnp.where(live, target * stride + place, devices * stride)
    words = position * CELLS + point_cell
    send_feats, packed = pack(words, point_feats, devices, capacity, stride)
    filled = jnp.arange(stride, dtype=jnp.int32)[None, :] < counts[:, None]
    send_cells = jnp.where(filled, packed[: devices * stride].reshape(devices, stride), -1)
    taps = conv_weight.transpose(0, 2, 1, 3).reshape(3 * channels, 3 * channels)
    return make_map(
        send_feats,
        send_cells.reshape(devices, 1, stride),
        taps,
        conv_bias.reshape(1, channels),
        size_gx,
        size_gy,
    )


def solution(mesh):
    in_specs = (
        P(("gx", "gy"), None),
        P(("gx", "gy"), None),
        P(("gx", "gy")),
        P(("gx", "gy")),
        P(),
        P(),
    )
    out_specs = (P("gx", "gy", None), P("gx", "gy", None))
    return jax.shard_map(shards, mesh=mesh, in_specs=in_specs, out_specs=out_specs, check_vma=False)
```

time: 149 us -> 116 us (0.78)
  Pallas kernels: 35.4 us -> 100 us
  waiting for transfers between devices: 63.5 us -> 0 us
  blocking collectives: 13.7 us -> 0 us
  starting transfers between devices: 12.6 us -> 0 us
  matrix products: 7.26 us -> 0.33 us
    pallas_call x1, Pallas kernels: 14.4 us -> 79.4 us  [make_map(): pl.pallas_call(functools.partial(map_kernel, size_gx, size_gy), out_shape...]
    all_to_all x1 -> x0, waiting for transfers between devices: 58.8 us -> none  [shards(): lax.all_to_all(send_feats, ('gx', 'gy'), split_axis=0, concat_axis=0, til...]
    all_to_all x1 -> x0, blocking collectives: 13.7 us -> none  [shards(): lax.all_to_all(send_cells[:devices * stride].reshape(devices, stride), ('...]
    ppermute x4 -> x0, starting transfers between devices: 9.41 us -> none  [the longest x2 5.71 us: with_halo(): lax.ppermute(tail, axis, [(i, (i + 1) % count) for i in range(ends)])]
    dot_general x9 -> x0, matrix products: 6.93 us -> none  [shards(): jnp.einsum('rcd,de->rce', window, conv_weight[shift_row, shift_col], pref...]
    broadcast_in_dim x1 -> x0, local copies, waits for them, and re-layouts: 4.91 us -> none  [shards(): rows = jnp.broadcast_to(rows.astype(jnp.bfloat16)[:, None], got_feats.shape)]
    ppermute x4 -> x0, waiting for transfers between devices: 4.68 us -> none  [the longest x2 4.68 us: with_halo(): lax.ppermute(head, axis, [((i + 1) % count, i) for i in range(ends)])]
    unnamed x15 -> x13, local copies, waits for them, and re-layouts: 2.29 us -> 6.16 us
  transfers between devices with their start and end apart: 5 -> 0, of which waited for: 3 -> 0; matrix products, arithmetic and copies ran while one was open for 2% -> 0% of each run, Pallas kernels for 0% -> 0%
where the time goes in v2:
time: 116 us; the launch traced here: 115 us
  Pallas kernels  100 us (86%)
  local copies, waits for them, and re-layouts  9.51 us (8%)
  other arithmetic  3.66 us (3%)
  between operations  1.42 us (1%)
    pallas_call x1, Pallas kernels, make_map(): pl.pallas_call(functools.partial(map_kernel, size_gx, size_gy), out_shape...  79.4 us
    pallas_call x1, Pallas kernels, pack(): pl.pallas_call(functools.partial(pack_kernel, stride), out_shape=(jax.Sha...  21 us
    unnamed x13, local copies, waits for them, and re-layouts  6.16 us

profile of v2, /device:TPU:1, one launch (start us, length us, event | category | flops | bytes accessed | tf_op | source)
XLA Modules:
  0.0 115.3 jit_solution(2843248668913170763)
XLA Ops:
  1.3 0.5 broadcast.28
  1.8 1.5 %fusion.9 = (s32[8192]{0:T(1024)S(1)}, s32[8192,1]{0,1:T(1,128)S(1)}) fusion(s32[8192,1]{0,1:T(1,128)} %param.7, s32[]{:T(128)} %broadcast.28), kind=kLoop, calls=%fused_computation.20 | loop fusion | flops 8192 | bytes 98308 | tf_op args[1]
  3.3 1.2 %copy.10 = bf16[3,128,3,128]{3,2,1,0:T(4,128)(2,1)S(1)} copy(bf16[3,128,3,128]{3,1,2,0:T(8,128)(2,1)} %bitcast.21) | data formatting | bytes 589824 | tf_op jit(solution)/shard_map/transpose | solution.py:316
  4.6 0.0 copy-start.3
  4.6 0.0 copy-start.1
  4.6 0.8 copy.14
  5.3 0.3 fusion.1
  5.7 0.4 slice_reduce_fusion
  6.0 0.2 reduce_window_sum.13
  6.2 0.2 fusion.8
  6.4 1.1 copy.9
  7.5 1.4 %subtract_reduce_fusion = f32[32,32]{1,0:T(8,128)S(1)} fusion(f32[32,32,1]{2,1,0:T(8,128)} %copy.9, f32[32,32,256]{2,1,0:T(8,128)S(1)} %fusion.1), kind=kLoop, calls=%fused_computation.4 | loop fusion | flops 1024 | bytes 12288 | tf_op jit(solution)/shard_map/sub | solution.py:295
  8.9 0.3 select_reduce_fusion
  9.2 0.0 copy-done.3
  9.3 0.0 copy-done.1
  9.3 21.0 %pack.1 = (bf16[32,320,128]{2,1,0:T(8,128)(2,1)S(1)}, s32[12672]{0:T(1024)S(1)}) custom-call(s32[8192]{0:T(1024)S(1)} %multiply_add_fusion.words, bf16[8192,128]{1,0:T(8,128)(2,1)S(1)} %copy-done.1), custom_call_target="tpu_custom_call" | custom-call | tf_op jit(solution)/shard_map/pack/pallas_call | solution.py:44
  30.2 0.0 copy-start
  30.3 1.5 %copy-done = bf16[32,320,128]{2,1,0:T(8,128)(2,1)} copy-done((bf16[32,320,128]{2,1,0:T(8,128)(2,1)}, bf16[32,320,128]{2,1,0:T(8,128)(2,1)S(1)}, u32[]{:S(2)}) %copy-start) | copy-done | bytes 2621464
  31.8 0.1 fusion.7
  31.9 0.7 reshape.49.send_cells
  32.5 79.4 %make_map.1 = (bf16[16,256,128]{2,1,0:T(8,128)(2,1)}, bf16[16,256,128]{2,1,0:T(8,128)(2,1)}) custom-call(bf16[32,320,128]{2,1,0:T(8,128)(2,1)} %copy-done, s32[32,1,384]{2,1,0:T(1,128)} %reshape.49.send_cells, bf16[384,384]{1,0:T(8,128)(2,1)} %bitcast.20, f32[1,128]{1,0:T(1,128)} %bitcast.25), custom_call_target="tpu_custom_call" | custom-call | tf_op jit(solution)/shard_map/make_map/pallas_call | solution.py:255
  111.9 0.0 copy-start.2
  111.9 2.4 %copy.18 = bf16[16,256,128]{2,1,0:T(8,128)(2,1)} copy(bf16[16,256,128]{2,1,0:T(8,128)(2,1)} %get-tuple-element.10) | data formatting | bytes 2097152
  114.3 0.0 copy-done.2
  114.3 1.0 copy.19
  (7 shorter events, 0.1 us)
Async XLA Ops:
  4.6 4.7 %copy-start.3 = (s32[8192]{0:T(1024)S(1)}, s32[8192]{0:T(1024)}, u32[]{:S(2)}) copy-start(s32[8192]{0:T(1024)} %param.8) | copy-start | bytes 98308
  4.6 4.7 %copy-start.1 = (bf16[8192,128]{1,0:T(8,128)(2,1)S(1)}, bf16[8192,128]{1,0:T(8,128)(2,1)}, u32[]{:S(2)}) copy-start(bf16[8192,128]{1,0:T(8,128)(2,1)} %feats.1) | copy-start | bytes 6291460
  30.2 1.5 %copy-start = (bf16[32,320,128]{2,1,0:T(8,128)(2,1)}, bf16[32,320,128]{2,1,0:T(8,128)(2,1)S(1)}, u32[]{:S(2)}) copy-start(bf16[32,320,128]{2,1,0:T(8,128)(2,1)S(1)} %get-tuple-element.4.send_feats) | copy-start | bytes 7864324
  111.9 2.4 %copy-start.2 = (bf16[16,256,128]{2,1,0:T(8,128)(2,1)S(1)}, bf16[16,256,128]{2,1,0:T(8,128)(2,1)}, u32[]{:S(2)}) copy-start(bf16[16,256,128]{2,1,0:T(8,128)(2,1)} %get-tuple-element.11) | copy-start | bytes 3145732

commit v3 on v2

--- a/solution.py
+++ b/solution.py
@@ -12,66 +12,27 @@
 CELLS = ROWS_DEV * COLS_DEV
 
 
-def pack_kernel(stride, words, feats, out, cells, fbuf, obuf):
-    points = feats.shape[0]
-    devices, capacity, _ = out.shape
-    step = 512
-
-    @pl.loop(0, points // step)
-    def _(i):
-        rows = pl.ds(pl.multiple_of(i * step, step), step)
-        fbuf[rows, :] = feats[rows, :].astype(jnp.float32)
-
-    @pl.loop(0, points // 16)
-    def _(i):
-        base = i * 16
-        for j in range(16):
-            word = words[base + j]
-            pos = lax.shift_right_logical(word, 12)
-            cells[pos] = word & (CELLS - 1)
-            obuf[pl.ds(pos, 1), :] = fbuf[pl.ds(base + j, 1), :]
-
-    @pl.loop(0, devices)
-    def _(t):
-        rows = pl.ds(pl.multiple_of(t * stride, stride), capacity)
-        out[t] = obuf[rows, :].astype(jnp.bfloat16)
-
-
-def pack(words, feats, devices, capacity, stride):
-    points, channels = feats.shape
-    smem = pl.BlockSpec(memory_space=pltpu.SMEM)
-    vmem = pl.BlockSpec(memory_space=pltpu.VMEM)
-    return pl.pallas_call(
-        functools.partial(pack_kernel, stride),
-        out_shape=(
-            jax.ShapeDtypeStruct((devices, capacity, channels), jnp.bfloat16),
-            jax.ShapeDtypeStruct(((devices + 1) * stride,), jnp.int32),
-        ),
-        in_specs=[smem, vmem],
-        out_specs=(vmem, smem),
-        scratch_shapes=[
-            pltpu.VMEM((points, channels), jnp.float32),
-            pltpu.VMEM((devices * stride + 8, channels), jnp.float32),
-        ],
-        compiler_params=pltpu.CompilerParams(vmem_limit_bytes=48 * 1024 * 1024),
-        name="pack",
-    )(words, feats)
-
-
 MESH = pl.DeviceIdType.MESH
 GROUP = 4
+CHUNK = 1024
 NEIGHBOURS = [(dx, dy) for dx in (-1, 0, 1) for dy in (-1, 0, 1) if (dx, dy) != (0, 0)]
 
 
 def map_kernel(
     size_gx,
     size_gy,
-    send_feats,
-    send_cells,
+    feats,
+    places,
+    keys,
     weight,
     bias,
     bev,
     conv,
+    slots,
+    tiles,
+    meta,
+    send_feats,
+    send_cells,
     got_feats,
     got_cells,
     acc,
@@ -105,6 +66,39 @@
             barrier, inc=1, device_id=(other // size_gy, lax.rem(other, size_gy)), device_id_type=MESH
         )
 
+    chunks = places.shape[0]
+    stride = got_feats.shape[1]
+
+    @pl.loop(0, chunks)
+    def _(c):
+        rows = pl.ds(pl.multiple_of(c * CHUNK, CHUNK), CHUNK)
+        ids = lax.broadcasted_iota(jnp.int32, (capacity, CHUNK), 0)
+        slots[c] = jnp.where(ids == places[c], 1.0, 0.0).astype(jnp.bfloat16)
+        key = jnp.transpose(jnp.broadcast_to(keys[c], (128, CHUNK))).astype(jnp.int32)
+        tile = jnp.right_shift(key, 12)
+        tiles[rows, :] = tile.astype(jnp.float32).astype(jnp.bfloat16)
+        hit = tile == lax.broadcasted_iota(jnp.int32, (CHUNK, 128), 1)
+        row = (jnp.right_shift(key, 8) & (ROWS_DEV - 1)) + 1
+        col = key & (COLS_DEV - 1)
+        for at, part in ((0, row), (128, col)):
+            part = jnp.where(hit, part, 0).astype(jnp.float32)
+            meta[rows, at : at + 128] = part.astype(jnp.bfloat16)
+
+    def packed(operand):
+        total = None
+        for c in range(chunks):
+            part = jnp.dot(slots[c], operand(c), preferred_element_type=jnp.float32)
+            total = part if total is None else total + part
+        return total
+
+    found = packed(lambda c: meta[c * CHUNK : (c + 1) * CHUNK, :])
+    found = found[:, :128] * 256.0 + found[:, 128:]
+    if stride > capacity:
+        found = jnp.concatenate([found, jnp.zeros((stride - capacity, 128), jnp.float32)], axis=0)
+    found = jnp.transpose(found)
+    for t in range(devices):
+        send_cells[t] = found[t : t + 1, :]
+
     pl.semaphore_wait(barrier, devices - 1)
 
     def copies(source, owner, target):
@@ -122,38 +116,74 @@
             ),
         )
 
-    @pl.loop(1, devices)
-    def _(k):
-        other = lax.rem(me + k, devices)
-        for copy in copies(other, me, other):
-            copy.start()
-
     mine = (
         pltpu.make_async_copy(send_cells.at[me], got_cells.at[me], own.at[0]),
         pltpu.make_async_copy(
             send_feats.at[me], got_feats.at[me, pl.ds(0, capacity)], own.at[1]
         ),
     )
-    for copy in mine:
-        copy.start()
+    pairs = devices // 2
+    half = me // 2
+
+    def send(q):
+        pair = lax.rem(half + q, pairs)
+        for k in range(2):
+            target = pair * 2 + k
+
+            @pl.when(target != me)
+            def _():
+                for copy in copies(target, me, target):
+                    copy.start()
+
+            @pl.when(target == me)
+            def _():
+                for copy in mine:
+                    copy.start()
+
+    @pl.loop(0, pairs)
+    def _(q):
+        pair = lax.rem(half + q, pairs)
+        names = [(pair * 2 + k).astype(jnp.float32).astype(jnp.bfloat16) for k in range(2)]
+
+        def masked(c):
+            rows = slice(c * CHUNK, (c + 1) * CHUNK)
+            values, tile = feats[rows, :], tiles[rows, :]
+            zero = jnp.zeros_like(values)
+            return jnp.concatenate([jnp.where(tile == n, values, zero) for n in names], axis=1)
+
+        block = packed(masked).astype(jnp.bfloat16)
+        for k in range(2):
+            send_feats[pair * 2 + k] = block[:, k * 128 : (k + 1) * 128]
+
+        @pl.when(q > 0)
+        def _():
+            send(q - 1)
+
+    send(pairs - 1)
     acc[...] = jnp.zeros_like(acc)
-    for copy in mine:
-        copy.wait()
 
     @pl.loop(0, devices // GROUP)
     def _(g):
-        owners = [lax.rem(me + devices - (g * GROUP + j), devices) for j in range(GROUP)]
-        for j, owner in enumerate(owners):
-
-            @pl.when(g * GROUP + j > 0)
+        owners = []
+        for j in range(GROUP // 2):
+            pair = lax.rem(half + pairs - (g * (GROUP // 2) + j), pairs)
+            owners += [pair * 2, pair * 2 + 1]
+        for owner in owners:
+
+            @pl.when(owner != me)
             def _():
                 for copy in copies(owner, owner, owner):
                     copy.wait_recv()
 
-        cells = jnp.concatenate([got_cells[owner] for owner in owners], axis=1)
+            @pl.when(owner == me)
+            def _():
+                for copy in mine:
+                    copy.wait()
+
+        cells = jnp.concatenate([got_cells[owner] for owner in owners], axis=1).astype(jnp.int32)
         values = jnp.concatenate([got_feats[owner] for owner in owners], axis=0)
         length = cells.shape[1]
-        row = jnp.right_shift(cells, 8).astype(jnp.float32)
+        row = (jnp.right_shift(cells, 8) - 1).astype(jnp.float32)
         row = jnp.transpose(jnp.broadcast_to(row, (128, length))).astype(jnp.bfloat16)
         col = cells & (COLS_DEV - 1)
         ids = lax.broadcasted_iota(jnp.int32, (COLS_DEV, length), 0)
@@ -246,20 +276,26 @@
             copy.wait_send()
 
 
-def make_map(feats, cells, weight, bias, size_gx, size_gy):
-    devices, capacity, channels = feats.shape
-    stride = cells.shape[-1]
+def make_map(feats, places, keys, weight, bias, size_gx, size_gy, capacity):
+    devices = size_gx * size_gy
+    points, channels = feats.shape
+    stride = -(-capacity // 128) * 128
     vmem = pl.BlockSpec(memory_space=pltpu.VMEM)
     shape = jax.ShapeDtypeStruct((ROWS_DEV, COLS_DEV, channels), jnp.bfloat16)
     dma = pltpu.SemaphoreType.DMA
     return pl.pallas_call(
         functools.partial(map_kernel, size_gx, size_gy),
         out_shape=(shape, shape),
-        in_specs=[vmem] * 4,
+        in_specs=[vmem] * 5,
         out_specs=(vmem, vmem),
         scratch_shapes=[
+            pltpu.VMEM((points // CHUNK, capacity, CHUNK), jnp.bfloat16),
+            pltpu.VMEM((points, 128), jnp.bfloat16),
+            pltpu.VMEM((points, 256), jnp.bfloat16),
+            pltpu.VMEM((devices, capacity, channels), jnp.bfloat16),
+            pltpu.VMEM((devices, 1, stride), jnp.float32),
             pltpu.VMEM((devices, stride, channels), jnp.bfloat16),
-            pltpu.VMEM((devices, 1, stride), jnp.int32),
+            pltpu.VMEM((devices, 1, stride), jnp.float32),
             pltpu.VMEM((COLS_DEV, ROWS_DEV * channels), jnp.float32),
             pltpu.VMEM((ROWS_DEV + 2, COLS_DEV, channels), jnp.bfloat16),
             pltpu.VMEM((2, ROWS_DEV, 1, channels), jnp.float32),
@@ -277,7 +313,7 @@
             collective_id=0, has_side_effects=True, vmem_limit_bytes=56 * 1024 * 1024
         ),
         name="make_map",
-    )(feats, cells, weight, bias)
+    )(feats, places, keys, weight, bias)
 
 
 def places(target, live, devices):
@@ -294,7 +330,7 @@
     running = jnp.cumsum(totals, axis=1)
     ranks = inner + (running - totals)[:, :, None]
     place = jnp.sum(jnp.where(hits.reshape(devices, nblk, blk), ranks, 0.0), axis=0)
-    return place.reshape(points).astype(jnp.int32) - 1, running[:, -1].astype(jnp.int32)
+    return place.reshape(points).astype(jnp.int32) - 1
 
 
 def shards(point_feats, point_tile, point_cell, point_count, conv_weight, conv_bias):
@@ -304,23 +340,20 @@
     points = point_feats.shape[0]
     channels = point_feats.shape[1]
     capacity = 5 * points // (4 * devices)
-    stride = -(-capacity // 128) * 128
     target = point_tile[:, 0]
     live = jnp.arange(points, dtype=jnp.int32) < point_count[0]
-    place, counts = places(target, live, devices)
-    position = jnp.where(live, target * stride + place, devices * stride)
-    words = position * CELLS + point_cell
-    send_feats, packed = pack(words, point_feats, devices, capacity, stride)
-    filled = jnp.arange(stride, dtype=jnp.int32)[None, :] < counts[:, None]
-    send_cells = jnp.where(filled, packed[: devices * stride].reshape(devices, stride), -1)
+    place = places(target, live, devices)
+    keys = jnp.where(live, target, devices) * CELLS + point_cell
     taps = conv_weight.transpose(0, 2, 1, 3).reshape(3 * channels, 3 * channels)
     return make_map(
-        send_feats,
-        send_cells.reshape(devices, 1, stride),
+        point_feats,
+        place.reshape(-1, 1, CHUNK),
+        keys.astype(jnp.float32).reshape(-1, 1, CHUNK),
         taps,
         conv_bias.reshape(1, channels),
         size_gx,
         size_gy,
+        capacity,
     )
 
 

time: 116 us -> 100 us (0.86)
  Pallas kernels: 100 us -> 87.5 us
  local copies, waits for them, and re-layouts: 9.51 us -> 6.71 us
    pallas_call x1 -> x0, Pallas kernels: 21 us -> none  [pack(): pl.pallas_call(functools.partial(pack_kernel, stride), out_shape=(jax.Sha...]
    pallas_call x1, Pallas kernels: 79.4 us -> 87.5 us  [make_map(): pl.pallas_call(functools.partial(map_kernel, size_gx, size_gy), out_shape...]
    unnamed x13 -> x6, local copies, waits for them, and re-layouts: 6.16 us -> 4.63 us
    convert_element_type x1, other arithmetic: 0.18 us -> 1.39 us  [shards(): keys.astype(jnp.float32).reshape(-1, 1, CHUNK)]
where the time goes in v3:
time: 100 us; the launch traced here: 99.9 us
  Pallas kernels  87.5 us (88%)
  local copies, waits for them, and re-layouts  6.71 us (7%)
  other arithmetic  3.96 us (4%)
  between operations  1.35 us (1%)
    pallas_call x1, Pallas kernels, make_map(): pl.pallas_call(functools.partial(map_kernel, size_gx, size_gy), out_shape...  87.5 us
    unnamed x6, local copies, waits for them, and re-layouts  4.63 us

profile of v3, /device:TPU:1, one launch (start us, length us, event | category | flops | bytes accessed | tf_op | source)
XLA Modules:
  0.0 99.9 jit_solution(6130210875705135636)
XLA Ops:
  1.3 0.5 broadcast.31
  1.8 1.5 %reduce.5 = s32[8192]{0:T(1024)S(1)} reduce(s32[8192,1]{0,1:T(1,128)} %param.7, s32[]{:T(128)} %broadcast.31), dimensions={1}, to_apply=%param.7.reduce_sub_computation.3 | reduce | bytes 65540 | tf_op args[1]
  3.3 1.4 %add_convert_fusion = f32[8192]{0:T(1024)} fusion(s32[8192]{0:T(1024)} %param.8, s32[8192]{0:T(1024)} %bitcast.20, s32[]{:T(128)} %bitcast.15), kind=kLoop, calls=%fused_computation.13 | loop fusion | flops 40960 | bytes 98308 | tf_op jit(solution)/shard_map/convert_element_type | solution.py:351
  4.7 1.2 %copy.13 = bf16[3,128,3,128]{3,2,1,0:T(4,128)(2,1)S(1)} copy(bf16[3,128,3,128]{3,1,2,0:T(8,128)(2,1)} %bitcast.18) | data formatting | bytes 589824 | tf_op jit(solution)/shard_map/transpose | solution.py:347
  5.9 0.8 copy.21
  6.7 0.3 fusion.1
  7.0 0.2 slice.4
  7.2 0.3 fusion.4
  7.5 0.5 fusion.3
  8.0 0.3 select_reduce_fusion
  8.3 0.6 sub.12.places
  9.0 87.5 %make_map.1 = (bf16[16,256,128]{2,1,0:T(8,128)(2,1)}, bf16[16,256,128]{2,1,0:T(8,128)(2,1)}) custom-call(bf16[8192,128]{1,0:T(8,128)(2,1)} %feats.1, s32[8,1,1024]{2,1,0:T(1,128)} %sub.12.places, f32[8,1,1024]{2,1,0:T(1,128)} %bitcast.19, bf16[384,384]{1,0:T(8,128)(2,1)} %bitcast.17, f32[1,128]{1,0:T(1,128)} %bitcast.21), custom_call_target="tpu_custom_call" | custom-call | tf_op jit(solution)/shard_map/make_map/pallas_call | solution.py:286
  96.5 0.0 copy-start
  96.5 2.4 %copy.25 = bf16[16,256,128]{2,1,0:T(8,128)(2,1)} copy(bf16[16,256,128]{2,1,0:T(8,128)(2,1)} %get-tuple-element.4) | data formatting | bytes 2097152
  98.9 0.0 copy-done
  98.9 1.0 copy.26
  (3 shorter events, 0.0 us)
Async XLA Ops:
  96.5 2.4 %copy-start = (bf16[16,256,128]{2,1,0:T(8,128)(2,1)S(1)}, bf16[16,256,128]{2,1,0:T(8,128)(2,1)}, u32[]{:S(2)}) copy-start(bf16[16,256,128]{2,1,0:T(8,128)(2,1)} %get-tuple-element.5) | copy-start | bytes 3145732

commit v4 on v3

--- a/solution.py
+++ b/solution.py
@@ -22,12 +22,12 @@
     size_gx,
     size_gy,
     feats,
-    places,
     keys,
-    weight,
+    taps,
     bias,
     bev,
     conv,
+    weight,
     slots,
     tiles,
     meta,
@@ -66,14 +66,31 @@
             barrier, inc=1, device_id=(other // size_gy, lax.rem(other, size_gy)), device_id_type=MESH
         )
 
-    chunks = places.shape[0]
+    chunks = keys.shape[0]
     stride = got_feats.shape[1]
 
-    @pl.loop(0, chunks)
-    def _(c):
+    for a in range(3):
+        for b in range(3):
+            weight[a * 128 : (a + 1) * 128, b * 128 : (b + 1) * 128] = taps[a, b]
+    inner = 256
+    upper = lax.broadcasted_iota(jnp.int32, (inner, inner), 0) <= lax.broadcasted_iota(
+        jnp.int32, (inner, inner), 1
+    )
+    upper = jnp.where(upper, 1.0, 0.0).astype(jnp.bfloat16)
+    names = lax.broadcasted_iota(jnp.int32, (devices, inner), 0)
+
+    def prepare(c, before):
+        target = jnp.right_shift(keys[c].astype(jnp.int32), 12)
+        found = []
+        for at in range(0, CHUNK, inner):
+            hits = jnp.where(names == target[:, at : at + inner], 1.0, 0.0)
+            ranks = jnp.dot(hits.astype(jnp.bfloat16), upper, preferred_element_type=jnp.float32)
+            found.append(jnp.sum(hits * (ranks + before), axis=0, keepdims=True) - 1.0)
+            before = before + jnp.sum(hits, axis=1, keepdims=True)
+        place = jnp.concatenate(found, axis=1).astype(jnp.int32)
         rows = pl.ds(pl.multiple_of(c * CHUNK, CHUNK), CHUNK)
         ids = lax.broadcasted_iota(jnp.int32, (capacity, CHUNK), 0)
-        slots[c] = jnp.where(ids == places[c], 1.0, 0.0).astype(jnp.bfloat16)
+        slots[c] = jnp.where(ids == place, 1.0, 0.0).astype(jnp.bfloat16)
         key = jnp.transpose(jnp.broadcast_to(keys[c], (128, CHUNK))).astype(jnp.int32)
         tile = jnp.right_shift(key, 12)
         tiles[rows, :] = tile.astype(jnp.float32).astype(jnp.bfloat16)
@@ -83,6 +100,9 @@
         for at, part in ((0, row), (128, col)):
             part = jnp.where(hit, part, 0).astype(jnp.float32)
             meta[rows, at : at + 128] = part.astype(jnp.bfloat16)
+        return before
+
+    lax.fori_loop(0, chunks, prepare, jnp.zeros((devices, inner), jnp.float32))
 
     def packed(operand):
         total = None
@@ -125,8 +145,11 @@
     pairs = devices // 2
     half = me // 2
 
+    def offset(q):
+        return lax.rem(2 * q + 1, pairs) - q // (pairs // 2)
+
     def send(q):
-        pair = lax.rem(half + q, pairs)
+        pair = lax.rem(half + offset(q), pairs)
         for k in range(2):
             target = pair * 2 + k
 
@@ -142,7 +165,7 @@
 
     @pl.loop(0, pairs)
     def _(q):
-        pair = lax.rem(half + q, pairs)
+        pair = lax.rem(half + offset(q), pairs)
         names = [(pair * 2 + k).astype(jnp.float32).astype(jnp.bfloat16) for k in range(2)]
 
         def masked(c):
@@ -166,7 +189,8 @@
     def _(g):
         owners = []
         for j in range(GROUP // 2):
-            pair = lax.rem(half + pairs - (g * (GROUP // 2) + j), pairs)
+            q = lax.rem(g * (GROUP // 2) + j + pairs // 2, pairs)
+            pair = lax.rem(half + pairs - offset(q), pairs)
             owners += [pair * 2, pair * 2 + 1]
         for owner in owners:
 
@@ -276,7 +300,7 @@
             copy.wait_send()
 
 
-def make_map(feats, places, keys, weight, bias, size_gx, size_gy, capacity):
+def make_map(feats, keys, weight, bias, size_gx, size_gy, capacity):
     devices = size_gx * size_gy
     points, channels = feats.shape
     stride = -(-capacity // 128) * 128
@@ -286,9 +310,10 @@
     return pl.pallas_call(
         functools.partial(map_kernel, size_gx, size_gy),
         out_shape=(shape, shape),
-        in_specs=[vmem] * 5,
+        in_specs=[vmem] * 4,
         out_specs=(vmem, vmem),
         scratch_shapes=[
+            pltpu.VMEM((3 * channels, 3 * channels), jnp.bfloat16),
             pltpu.VMEM((points // CHUNK, capacity, CHUNK), jnp.bfloat16),
             pltpu.VMEM((points, 128), jnp.bfloat16),
             pltpu.VMEM((points, 256), jnp.bfloat16),
@@ -313,24 +338,7 @@
             collective_id=0, has_side_effects=True, vmem_limit_bytes=56 * 1024 * 1024
         ),
         name="make_map",
-    )(feats, places, keys, weight, bias)
-
-
-def places(target, live, devices):
-    points = target.shape[0]
-    blk = 256
-    nblk = points // blk
-    tile_ids = jnp.arange(devices, dtype=jnp.int32)
-    hits = (tile_ids[:, None] == target[None, :]) & live[None, :]
-    inner_idx = jnp.arange(blk, dtype=jnp.int32)
-    upper = (inner_idx[:, None] <= inner_idx[None, :]).astype(jnp.bfloat16)
-    blocks = hits.astype(jnp.bfloat16).reshape(devices, nblk, blk)
-    inner = jnp.einsum("dbj,ji->dbi", blocks, upper, preferred_element_type=jnp.float32)
-    totals = inner[:, :, -1]
-    running = jnp.cumsum(totals, axis=1)
-    ranks = inner + (running - totals)[:, :, None]
-    place = jnp.sum(jnp.where(hits.reshape(devices, nblk, blk), ranks, 0.0), axis=0)
-    return place.reshape(points).astype(jnp.int32) - 1
+    )(feats, keys, weight, bias)
 
 
 def shards(point_feats, point_tile, point_cell, point_count, conv_weight, conv_bias):
@@ -342,14 +350,11 @@
     capacity = 5 * points // (4 * devices)
     target = point_tile[:, 0]
     live = jnp.arange(points, dtype=jnp.int32) < point_count[0]
-    place = places(target, live, devices)
     keys = jnp.where(live, target, devices) * CELLS + point_cell
-    taps = conv_weight.transpose(0, 2, 1, 3).reshape(3 * channels, 3 * channels)
     return make_map(
         point_feats,
-        place.reshape(-1, 1, CHUNK),
         keys.astype(jnp.float32).reshape(-1, 1, CHUNK),
-        taps,
+        conv_weight,
         conv_bias.reshape(1, channels),
         size_gx,
         size_gy,

time: 100 us -> 93.1 us (0.931)
  local copies, waits for them, and re-layouts: 6.71 us -> 3.36 us
  other arithmetic: 3.96 us -> 1.4 us
    unnamed x1 -> x0, other arithmetic: 1.48 us -> none
    unnamed x6 -> x4, local copies, waits for them, and re-layouts: 4.63 us -> 3.36 us
    transpose x1 -> x0, local copies, waits for them, and re-layouts: 1.22 us -> none  [shards(): taps = conv_weight.transpose(0, 2, 1, 3).reshape(3 * channels, 3 * channels)]
where the time goes in v4:
time: 93.1 us; the launch traced here: 92.9 us
  Pallas kernels  86.8 us (93%)
  local copies, waits for them, and re-layouts  3.36 us (4%)
  other arithmetic  1.4 us (2%)
  between operations  1.29 us (1%)
    pallas_call x1, Pallas kernels, make_map(): pl.pallas_call(functools.partial(map_kernel, size_gx, size_gy), out_shape...  86.8 us
    unnamed x4, local copies, waits for them, and re-layouts  3.36 us

profile of v4, /device:TPU:1, one launch (start us, length us, event | category | flops | bytes accessed | tf_op | source)
XLA Modules:
  0.0 92.9 jit_solution(952914596395187928)
XLA Ops:
  1.3 1.4 %add_convert_fusion = f32[8192]{0:T(1024)} fusion(s32[8192]{0:T(1024)} %param.8, s32[8192]{0:T(1024)} %bitcast.6, s32[]{:T(128)} %bitcast.4), kind=kLoop, calls=%fused_computation | loop fusion | flops 40960 | bytes 98308 | tf_op jit(solution)/shard_map/convert_element_type | solution.py:356
  2.7 86.8 %make_map.1 = (bf16[16,256,128]{2,1,0:T(8,128)(2,1)}, bf16[16,256,128]{2,1,0:T(8,128)(2,1)}) custom-call(bf16[8192,128]{1,0:T(8,128)(2,1)} %feats.1, f32[8,1,1024]{2,1,0:T(1,128)} %bitcast.5, bf16[3,3,128,128]{3,2,1,0:T(8,128)(2,1)} %taps.1, f32[1,128]{1,0:T(1,128)} %bitcast.7), custom_call_target="tpu_custom_call" | custom-call | tf_op jit(solution)/shard_map/make_map/pallas_call | solution.py:310
  89.5 0.0 copy-start
  89.5 2.4 %copy.11 = bf16[16,256,128]{2,1,0:T(8,128)(2,1)} copy(bf16[16,256,128]{2,1,0:T(8,128)(2,1)} %get-tuple-element.4) | data formatting | bytes 2097152
  91.9 0.0 copy-done
  91.9 1.0 %copy.12 = bf16[16,256,128]{2,1,0:T(8,128)(2,1)} copy(bf16[16,256,128]{2,1,0:T(8,128)(2,1)S(1)} %copy-done) | data formatting | bytes 2097152
Async XLA Ops:
  89.5 2.4 %copy-start = (bf16[16,256,128]{2,1,0:T(8,128)(2,1)S(1)}, bf16[16,256,128]{2,1,0:T(8,128)(2,1)}, u32[]{:S(2)}) copy-start(bf16[16,256,128]{2,1,0:T(8,128)(2,1)} %get-tuple-element.5) | copy-start | bytes 3145732
